TPU v7x, 32 devices: a whole 2x2x4 slice. The times are simulated.
32 devices in a mesh: dp: 8 (over y, x, core), mp: 4 (over z).
Axes of the slice: x: 2, y: 2, z: 4, core: 2. Of those that a mesh axis runs over, the one named last changes fastest.
Arguments:
- acts: bfloat16 [4096, 3072], P('dp'), may hold values from -16 to 16
- grads_out: bfloat16 [4096, 8192], P('dp', 'mp'), may hold values from -0.125 to 0.125
- old_a: float32 [8, 3, 128, 1024], P('dp'), may hold values from -0.09375 to 0.09375
- old_g: float32 [4, 8, 2, 128, 1024], P('mp', 'dp'), may hold values from -0.09375 to 0.09375
- a_inverse: bfloat16 [3072, 1024], P('dp'), may hold values from -0.1875 to 0.1875
- g_inverse: bfloat16 [8192, 1024], P('mp'), may hold values from -0.1875 to 0.1875
- owner_map: int32 [5, 8], replicated, may hold values from 0 to 7, each once within a row
Outputs:
- a_factor: float32 [8, 3, 128, 1024], P('dp')
- g_factor: float32 [4, 8, 2, 128, 1024], P('mp', 'dp')
- preconditioned: bfloat16 [3072, 4, 2048], P(None, 'mp', 'dp')
Inputs may be any that keep to these rules, and one draw needn't show every extreme that they name: `owner_map`: each row is a permutation: row k tells, for each of the 8 row strips of factor block k, which dp index holds it. Rows 0 to 2 are the activation blocks, the others the output-gradient blocks of every mp index.
All inputs are finite; a program needn't handle non-finite values.
Results may differ from a plain program's by a relative error of at most 0.02.
Values may be sent and summed in bfloat16 or wider, within the bound.
A program may use at most 128 MiB of HBM per device.

v0:
```python
import jax
import jax.numpy as jnp
from jax import lax
from jax.sharding import PartitionSpec as P

D_WIN = 3072
BLOCK = 1024
FF_DEV = 2048
TOK_DEV = 512
NA = 3
NG = 2
decay_rate = 0.75


def to_owner(stacked, where_from):
    return jnp.take_along_axis(stacked, where_from[:, :, None, None], axis=1)


def per_device(acts, grads_out, old_a, old_g, a_inverse, g_inverse, owner_map):
    dp_count = lax.axis_size("dp")
    mp_count = lax.axis_size("mp")
    tokens = acts.shape[0] * dp_count
    strip_rows = BLOCK // dp_count
    owners = jnp.arange(dp_count, dtype=jnp.int32)
    matches = owner_map[:, :, None] == owners[None, None, :]
    where_from = jnp.sum(jnp.where(matches, owners[None, :, None], 0), axis=1)
    blocks_a = acts.reshape(TOK_DEV, NA, BLOCK)
    blocks_g = grads_out.reshape(TOK_DEV, NG, BLOCK)
    sub_rows = strip_rows // mp_count
    row_split = blocks_a.reshape(TOK_DEV, NA, dp_count, mp_count, sub_rows)
    own_rows = lax.dynamic_index_in_dim(row_split, lax.axis_index("mp"), axis=3, keepdims=False)
    a_partial = (
        jnp.einsum("tksr,tkc->ksrc", own_rows, blocks_a, preferred_element_type=jnp.float32)
        / tokens
    )
    g_partial = jnp.einsum("tkb,tkc->kbc", blocks_g, blocks_g, preferred_element_type=jnp.float32)
    g_partial = g_partial.reshape(NG, dp_count, strip_rows, BLOCK)
    a_sent = to_owner(a_partial, where_from[:NA])
    g_sent = to_owner(g_partial, where_from[NA:])
    summed = (
        lax.psum_scatter(a_sent.astype(jnp.bfloat16), "dp", scatter_dimension=1, tiled=True).astype(
            jnp.float32
        ),
        lax.psum_scatter(g_sent.astype(jnp.bfloat16), "dp", scatter_dimension=1, tiled=True).astype(
            jnp.float32
        ),
    )
    a_cov = summed[0]
    a_cov = lax.all_gather(a_cov.astype(jnp.bfloat16), "mp", axis=2, tiled=True).astype(a_cov.dtype)
    g_cov = summed[1]
    a_factor = decay_rate * old_a + (1.0 - decay_rate) * a_cov.reshape(old_a.shape)
    g_factor = decay_rate * old_g + (1.0 - decay_rate) * g_cov.reshape(old_g.shape)
    rows_dev = acts.shape[1] // dp_count
    grad_sum = lax.psum_scatter(
        lax.dot_general(
            acts, grads_out, (((0,), (0,)), ((), ())), preferred_element_type=jnp.float32
        ).astype(jnp.bfloat16),
        "dp",
        scatter_dimension=0,
        tiled=True,
    )
    grad_low = grad_sum.reshape(rows_dev, NG, BLOCK)
    g_blocks = g_inverse.reshape(NG, BLOCK, BLOCK)
    right_done = jnp.einsum("rjb,jbc->rjc", grad_low, g_blocks, preferred_element_type=jnp.float32)
    right_done = right_done.astype(jnp.bfloat16).reshape(rows_dev, FF_DEV)
    column_strip = lax.all_to_all(right_done, "dp", split_axis=1, concat_axis=0, tiled=True)
    inverse_all = lax.all_gather(a_inverse, "dp", axis=0, tiled=True).reshape(NA, BLOCK, BLOCK)
    result = jnp.einsum(
        "kbc,kcf->kbf",
        inverse_all,
        column_strip.reshape(NA, BLOCK, -1),
        preferred_element_type=jnp.float32,
    )
    result = result.astype(jnp.bfloat16).reshape(D_WIN, 1, -1)
    return (a_factor, g_factor, result)


def solution(mesh):
    placed = (
        P("dp", None),
        P("dp", "mp"),
        P("dp", None, None, None),
        P("mp", "dp", None, None, None),
        P("dp", None),
        P("mp", None),
        P(),
    )
    return jax.shard_map(
        per_device,
        mesh=mesh,
        in_specs=placed,
        out_specs=(P("dp", None, None, None), P("mp", "dp", None, None, None), P(None, "mp", "dp")),
        check_vma=False,
    )
```

profile of v0, /device:TPU:0, one launch (start us, length us, event | category | flops | bytes accessed | tf_op | source)
XLA Modules:
  0.0 317.3 jit_solution(11359047946663445373)
XLA Ops:
  7.2 0.0 reduce-scatter.8.cloned.1.call-start
  7.2 11.7 %convolution_convert_fusion = bf16[3072,2048]{1,0:T(8,128)(2,1)} fusion(bf16[512,3072]{1,0:T(8,128)(2,1)} %param.7, bf16[512,2048]{1,0:T(8,128)(2,1)} %param.8), kind=kOutput, calls=%fused_computation.2 | convolution fusion | flops 6448742400 | bytes 17825792 | tf_op jit(solution)/shard_map/dot_general | solution.py:55
  18.9 0.0 copy-start.1
  18.9 0.0 copy-start.2
  18.9 0.0 reduce-scatter.8.cloned.1.call-update
  18.9 0.0 all-reduce.3.cloned.1.call-start
  19.0 0.6 copy-done.1
  19.6 0.1 select_reduce_fusion
  19.7 0.1 reshape.123
  19.8 0.7 copy-done.2
  20.5 4.4 %fusion.1 = bf16[2,1024,1024]{2,1,0:T(8,128)(2,1)} fusion(bf16[64,2,8,1024]{3,2,1,0:T(8,128)(2,1)S(1)} %bitcast.67), kind=kOutput, calls=%fused_computation.6 | convolution fusion | flops 2147483648 | bytes 6291456 | tf_op jit(solution)/shard_map/tkb,tkc->kbc/dot_general | solution.py:36
  24.9 5.0 %gather_fusion.1 = bf16[16,128,1024]{2,1,0:T(8,128)(2,1)} fusion(bf16[2,8,128,1024]{3,2,1,0:T(8,128)(2,1)} %bitcast.62, s32[16]{0:T(128)S(1)} %reshape.123), kind=kCustom, calls=%fused_computation.1 | custom fusion | bytes 8388736 | tf_op jit(solution)/shard_map/jit(take_along_axis)/gather | solution.py:16
  29.8 7.6 %select_convert_fusion = bf16[2,8,128,1024]{3,2,1,0:T(8,128)(2,1)} fusion(bf16[2,8,128,1024]{3,2,1,0:T(8,128)(2,1)} %bitcast.57, pred[2,8]{1,0:T(4,128)(4,1)S(1)} %compare_and_fusion), kind=kLoop, calls=%fused_computation.3 | loop fusion | flops 2097152 | bytes 8388624 | tf_op jit(solution)/shard_map/convert_element_type | solution.py:44
  37.4 0.0 all-reduce.3.cloned.1.call-update
  37.5 0.0 reduce-scatter.6.cloned.1.call-start
  37.5 3.6 %copy.43 = bf16[512,3072]{0,1:T(8,128)(2,1)S(1)} copy(bf16[512,3072]{1,0:T(8,128)(2,1)} %param.7) | data formatting | bytes 6291456 | tf_op args[0]
  41.1 0.1 reshape.117
  41.2 0.1 copy.42
  41.3 2.2 convolution_multiply_fusion
  43.5 2.1 gather_fusion
  45.6 1.7 fusion
  47.3 0.0 reduce-scatter.6.cloned.1.call-update
  47.3 0.0 all-gather.2.cloned.1.call-start
  47.3 0.5 all-gather.2.cloned.1.call-update
  47.9 66.2 %reduce-scatter.8.cloned.1.call-done = bf16[384,2048]{1,0:T(8,128)(2,1)} async-done(((bf16[3072,2048]{1,0:T(8,128)(2,1)}), bf16[384,2048]{1,0:T(8,128)(2,1)}) %reduce-scatter.8.cloned.1.call-update) | async-done | bytes 1572880 | tf_op jit(solution)/shard_map/reduce_scatter | solution.py:54
  114.1 4.5 %fusion.7 = bf16[384,2,1024]{2,0,1:T(8,128)(2,1)S(1)} fusion(bf16[2,1024,1024]{2,1,0:T(8,128)(2,1)} %bitcast.66, bf16[48,2,8,1024]{3,2,1,0:T(8,128)(2,1)} %bitcast.68), kind=kOutput, calls=%fused_computation.16 | convolution fusion | flops 1611399168 | bytes 7340032 | tf_op jit(solution)/shard_map/rjb,jbc->rjc/dot_general | solution.py:64
  118.5 1.6 copy.50
  120.1 0.0 copy-start.3
  120.1 3.8 %all-to-all-start = ((bf16[384,8,256]{0,2,1:T(8,128)(2,1)}), bf16[384,8,256]{0,2,1:T(8,128)(2,1)S(1)}, u32[]{:S(2)}, u32[]{:S(2)}) async-start(bf16[384,8,256]{0,2,1:T(8,128)(2,1)} %bitcast.13), calls=%async_computation.2 | async-start | bytes 3145728 | tf_op jit(solution)/shard_map/all_to_all | solution.py:66
  123.9 0.0 copy-start
  123.9 0.0 copy-done.3
  124.0 0.6 dynamic-slice
  124.5 90.5 %all-reduce.3.cloned.1.call-done = bf16[2,8,128,1024]{3,2,1,0:T(8,128)(2,1)} async-done(((bf16[2,8,128,1024]{3,2,1,0:T(8,128)(2,1)}), bf16[2,8,128,1024]{3,2,1,0:T(8,128)(2,1)}) %all-reduce.3.cloned.1.call-update) | async-done | bytes 4194320
  215.0 3.2 bitcast_add_fusion.1
  218.2 39.1 %reduce-scatter.6.cloned.1.call-done = bf16[3,1,32,1024]{3,2,0,1:T(8,128)(2,1)} async-done(((bf16[3,8,32,1024]{3,2,0,1:T(8,128)(2,1)}), bf16[3,1,32,1024]{3,2,0,1:T(8,128)(2,1)}) %reduce-scatter.6.cloned.1.call-update) | async-done | bytes 196624 | tf_op jit(solution)/shard_map/reduce_scatter | solution.py:41
  257.3 19.9 %all_gather.6 = bf16[3,1,128,1024]{3,2,0,1:T(8,128)(2,1)S(1)} all-gather(bf16[3,1,32,1024]{3,2,0,1:T(8,128)(2,1)} %reduce-scatter.6.cloned.1.call-done), channel_id=1, replica_groups=mesh['dp'=8,'mp'=4] {'mp'}, dimensions={2}, use_global_device_ids=true | all-gather | bytes 983040 | tf_op jit(solution)/shard_map/all_gather | solution.py:49
  277.3 0.0 copy-done
  277.3 1.4 bitcast_add_fusion
  278.7 0.0 all-to-all-done
  278.7 0.7 copy.51
  279.5 25.0 %all-gather.2.cloned.1.call-done = bf16[3072,1024]{1,0:T(8,128)(2,1)} async-done(((bf16[384,1024]{1,0:T(8,128)(2,1)}), bf16[3072,1024]{1,0:T(8,128)(2,1)}) %all-gather.2.cloned.1.call-update) | async-done | bytes 6291472 | tf_op jit(solution)/shard_map/all_gather | solution.py:67
  304.5 4.7 %fusion.6 = bf16[3,1024,256]{1,2,0:T(8,128)(2,1)S(1)} fusion(bf16[3,1024,256]{2,1,0:T(8,128)(2,1)S(1)} %bitcast.64, bf16[3,1024,1024]{2,1,0:T(8,128)(2,1)} %bitcast.65), kind=kOutput, calls=%fused_computation.15 | convolution fusion | flops 1611399168 | bytes 9437184 | tf_op jit(solution)/shard_map/kbc,kcf->kbf/dot_general | solution.py:68
  309.2 1.6 copy.53
  (4 shorter events, 0.0 us)
Async XLA Ops:
  7.2 106.9 %reduce-scatter.8.cloned.1.call-start = ((), (), s32[]{:S(2)}) async-start(), calls=%async_computation.4 | async-start | bytes 14155776 | tf_op jit(solution)/shard_map/reduce_scatter | solution.py:54
  18.9 0.7 copy-start.1
  18.9 1.6 copy-start.2
  18.9 196.1 %all-reduce.3.cloned.1.call-start = ((), (), s32[]{:S(2)}) async-start(), calls=%async_computation.6 | async-start | bytes 8388608
  37.5 219.9 %reduce-scatter.6.cloned.1.call-start = ((), (), s32[]{:S(2)}) async-start(), calls=%async_computation.3 | async-start | bytes 1769472 | tf_op jit(solution)/shard_map/reduce_scatter | solution.py:41
  47.3 257.2 %all-gather.2.cloned.1.call-start = ((), (), s32[]{:S(2)}) async-start(), calls=%async_computation.5 | async-start | bytes 7077888 | tf_op jit(solution)/shard_map/all_gather | solution.py:67
  120.1 3.8 %copy-start.3 = (u32[32]{0:T(128)S(1)}, u32[32]{0:T(128)}, u32[]{:S(2)}) copy-start(u32[32]{0:T(128)} %constant.77) | copy-start | bytes 388
  120.1 158.6 %all-to-all-start = ((bf16[384,8,256]{0,2,1:T(8,128)(2,1)}), bf16[384,8,256]{0,2,1:T(8,128)(2,1)S(1)}, u32[]{:S(2)}, u32[]{:S(2)}) async-start(bf16[384,8,256]{0,2,1:T(8,128)(2,1)} %bitcast.13), calls=%async_computation.2 | async-start | bytes 3145728 | tf_op jit(solution)/shard_map/all_to_all | solution.py:66
  123.9 153.3 %copy-start = (f32[1,3,128,1024]{3,2,1,0:T(8,128)S(1)}, f32[1,3,128,1024]{3,2,1,0:T(8,128)}, u32[]{:S(2)}) copy-start(f32[1,3,128,1024]{3,2,1,0:T(8,128)} %param.9) | copy-start | bytes 4718596
Sparse Core Ops, SparseCore 0:
  19.0 94.9 reduce-scatter.7
  117.3 97.6 all-reduce.2
  218.9 38.3 reduce-scatter.5
  259.1 45.3 all-gather.1
where the time goes:
time: 318 us; the launch traced here: 317 us
  waiting for transfers between devices  221 us (69%)
  matrix products  27.4 us (9%)
  blocking collectives  19.9 us (6%)
  local copies, waits for them, and re-layouts  16.7 us (5%)
  other arithmetic  14 us (4%)
  between operations  13.9 us (4%)
  starting transfers between devices  3.97 us (1%)
    unnamed x5, waiting for transfers between devices  91 us
    reduce_scatter x1, waiting for transfers between devices, per_device(): lax.psum_scatter(lax.dot_general(acts, grads_out, (((0,), (0,)), ((), ())...  66.2 us
    reduce_scatter x1, waiting for transfers between devices, per_device(): lax.psum_scatter(a_sent.astype(jnp.bfloat16), 'dp', scatter_dimension=1,...  39.1 us
    all_gather x1, waiting for transfers between devices, per_device(): lax.all_gather(a_inverse, 'dp', axis=0, tiled=True)  25 us
    all_gather x1, blocking collectives, per_device(): lax.all_gather(a_cov.astype(jnp.bfloat16), 'mp', axis=2, tiled=True)  19.9 us
    dot_general x1, matrix products, per_device(): lax.dot_general(acts, grads_out, (((0,), (0,)), ((), ())), preferred_elem...  11.7 us
    convert_element_type x1, other arithmetic, per_device(): g_sent.astype(jnp.bfloat16)  7.62 us
    gather x4, local copies, waits for them, and re-layouts, to_owner(): return jnp.take_along_axis(stacked, where_from[:, :, None, None], axis=1)  7.19 us
  transfers between devices with their start and end apart: 5, of which 4 were waited for; matrix products, arithmetic and copies ran while one was open for 12% of the time, Pallas kernels for 0%

commit v1 on v0

--- a/solution.py
+++ b/solution.py
@@ -1,7 +1,9 @@
+import functools
 import jax
 import jax.numpy as jnp
 from jax import lax
 from jax.sharding import PartitionSpec as P
+from jax.lax import all_gather
 
 D_WIN = 3072
 BLOCK = 1024
@@ -10,6 +12,14 @@
 NA = 3
 NG = 2
 decay_rate = 0.75
+
+
+def _edit_ticks(q_in, axis_key):
+    x_next = jnp.concatenate(all_gather(q_in, axis_key), axis=2)
+    return x_next
+
+
+ways_match = functools.partial(_edit_ticks, axis_key="mp")
 
 
 def to_owner(stacked, where_from):
@@ -46,7 +56,7 @@
         ),
     )
     a_cov = summed[0]
-    a_cov = lax.all_gather(a_cov.astype(jnp.bfloat16), "mp", axis=2, tiled=True).astype(a_cov.dtype)
+    a_cov = ways_match(a_cov.astype(jnp.bfloat16)).astype(a_cov.dtype)
     g_cov = summed[1]
     a_factor = decay_rate * old_a + (1.0 - decay_rate) * a_cov.reshape(old_a.shape)
     g_factor = decay_rate * old_g + (1.0 - decay_rate) * g_cov.reshape(old_g.shape)

time: 318 us -> 294 us (0.925)
  waiting for transfers between devices: 221 us -> 194 us
  matrix products: 27.4 us -> 30.8 us
    reduce_scatter x1 -> x0, waiting for transfers between devices: 39.1 us -> none  [per_device(): lax.psum_scatter(a_sent.astype(jnp.bfloat16), 'dp', scatter_dimension=1,...]
    unnamed x5 -> x4, waiting for transfers between devices: 91 us -> 109 us
    all_gather x1, waiting for transfers between devices: 25 us -> 19.6 us  [per_device(): lax.all_gather(a_inverse, 'dp', axis=0, tiled=True)]
    dot_general x1, matrix products: 4.36 us -> 7.83 us  [per_device(): jnp.einsum('tkb,tkc->kbc', blocks_g, blocks_g, preferred_element_type=jnp...]
    unnamed x10 -> x11, local copies, waits for them, and re-layouts: 5.52 us -> 6.42 us
  transfers between devices with their start and end apart: 5 -> 4, of which waited for: 4 -> 3; matrix products, arithmetic and copies ran while one was open for 12% -> 15% of each run, Pallas kernels for 0% -> 0%
where the time goes in v1:
time: 294 us; the launch traced here: 293 us
  waiting for transfers between devices  194 us (66%)
  matrix products  30.8 us (10%)
  blocking collectives  19.7 us (7%)
  local copies, waits for them, and re-layouts  18.8 us (6%)
  between operations  13.9 us (5%)
  other arithmetic  12 us (4%)
  starting transfers between devices  3.83 us (1%)
    unnamed x4, waiting for transfers between devices  109 us
    reduce_scatter x1, waiting for transfers between devices, per_device(): lax.psum_scatter(lax.dot_general(acts, grads_out, (((0,), (0,)), ((), ())...  65.2 us
    all_gather x1, blocking collectives, _edit_ticks(): x_next = jnp.concatenate(all_gather(q_in, axis_key), axis=2)  19.7 us
    all_gather x1, waiting for transfers between devices, per_device(): lax.all_gather(a_inverse, 'dp', axis=0, tiled=True)  19.6 us
    dot_general x1, matrix products, per_device(): lax.dot_general(acts, grads_out, (((0,), (0,)), ((), ())), preferred_elem...  11.7 us
    gather x4, local copies, waits for them, and re-layouts, to_owner(): return jnp.take_along_axis(stacked, where_from[:, :, None, None], axis=1)  8.35 us
    dot_general x1, matrix products, per_device(): jnp.einsum('tkb,tkc->kbc', blocks_g, blocks_g, preferred_element_type=jnp...  7.83 us
    unnamed x11, local copies, waits for them, and re-layouts  6.42 us
  transfers between devices with their start and end apart: 4, of which 3 were waited for; matrix products, arithmetic and copies ran while one was open for 15% of the time, Pallas kernels for 0%

profile of v1, /device:TPU:0, one launch (start us, length us, event | category | flops | bytes accessed | tf_op | source)
XLA Modules:
  0.0 293.3 jit_solution(820730358544375701)
XLA Ops:
  7.2 0.0 reduce-scatter.8.cloned.1.call-start
  7.2 11.7 %convolution_convert_fusion = bf16[3072,2048]{1,0:T(8,128)(2,1)} fusion(bf16[512,3072]{1,0:T(8,128)(2,1)} %param.7, bf16[512,2048]{1,0:T(8,128)(2,1)} %param.8), kind=kOutput, calls=%fused_computation.2 | convolution fusion | flops 6448742400 | bytes 17825792 | tf_op jit(solution)/shard_map/dot_general | solution.py:65
  18.9 0.0 reduce-scatter.8.cloned.1.call-update
  18.9 0.0 all-reduce.5.cloned.1.call-start
  19.0 0.0 copy-start.2
  19.0 3.2 %copy.39 = bf16[512,3072]{0,1:T(8,128)(2,1)S(1)} copy(bf16[512,3072]{1,0:T(8,128)(2,1)} %param.7) | data formatting | bytes 6291456 | tf_op args[0]
  22.2 0.0 copy-done.2
  22.2 0.1 select_reduce_fusion
  22.3 0.1 reshape.127
  22.4 0.1 reshape.133
  22.5 2.2 convolution_multiply_fusion
  24.6 2.1 gather_fusion
  26.7 7.8 %fusion = bf16[2,1024,1024]{2,1,0:T(8,128)(2,1)} fusion(bf16[64,2,8,1024]{3,2,1,0:T(8,128)(2,1)} %bitcast.77), kind=kOutput, calls=%fused_computation.5 | convolution fusion | flops 2147483648 | bytes 6291456 | tf_op jit(solution)/shard_map/tkb,tkc->kbc/dot_general | solution.py:46
  34.5 6.1 %gather_fusion.1 = bf16[16,128,1024]{2,1,0:T(8,128)(2,1)} fusion(bf16[2,8,128,1024]{3,2,1,0:T(8,128)(2,1)} %bitcast.72, s32[16]{0:T(128)S(1)} %reshape.133), kind=kCustom, calls=%fused_computation.1 | custom fusion | bytes 8388736 | tf_op jit(solution)/shard_map/jit(take_along_axis)/gather | solution.py:26
  40.7 1.7 select_convert_fusion.1
  42.4 5.8 %select_convert_fusion = bf16[2,8,128,1024]{3,2,1,0:T(8,128)(2,1)} fusion(bf16[2,8,128,1024]{3,2,1,0:T(8,128)(2,1)} %bitcast.66, pred[2,8]{1,0:T(4,128)(4,1)S(1)} %compare_and_fusion), kind=kLoop, calls=%fused_computation.3 | loop fusion | flops 2097152 | bytes 8388624 | tf_op jit(solution)/shard_map/convert_element_type | solution.py:54
  48.1 0.0 all-reduce.5.cloned.1.call-update
  48.2 0.0 all-gather.3.cloned.1.call-start
  48.2 0.7 all-gather.3.cloned.1.call-update
  48.9 65.2 %reduce-scatter.8.cloned.1.call-done = bf16[384,2048]{1,0:T(8,128)(2,1)} async-done(((bf16[3072,2048]{1,0:T(8,128)(2,1)}), bf16[384,2048]{1,0:T(8,128)(2,1)}) %reduce-scatter.8.cloned.1.call-update) | async-done | bytes 1572880 | tf_op jit(solution)/shard_map/reduce_scatter | solution.py:64
  114.1 4.5 %fusion.6 = bf16[384,2,1024]{2,0,1:T(8,128)(2,1)S(1)} fusion(bf16[2,1024,1024]{2,1,0:T(8,128)(2,1)} %bitcast.76, bf16[48,2,8,1024]{3,2,1,0:T(8,128)(2,1)} %bitcast.78), kind=kOutput, calls=%fused_computation.16 | convolution fusion | flops 1611399168 | bytes 7340032 | tf_op jit(solution)/shard_map/rjb,jbc->rjc/dot_general | solution.py:74
  118.5 1.6 copy.46
  120.1 0.0 copy-start.3
  120.1 3.7 %all-to-all-start = ((bf16[384,8,256]{0,2,1:T(8,128)(2,1)}), bf16[384,8,256]{0,2,1:T(8,128)(2,1)S(1)}, u32[]{:S(2)}, u32[]{:S(2)}) async-start(bf16[384,8,256]{0,2,1:T(8,128)(2,1)} %bitcast.15), calls=%async_computation.1 | async-start | bytes 3145728 | tf_op jit(solution)/shard_map/all_to_all | solution.py:76
  123.8 0.0 copy-done.3
  123.8 0.6 dynamic-slice
  124.4 108.7 %all-reduce.5.cloned.1.call-done = (bf16[3,8,32,1024]{3,2,1,0:T(8,128)(2,1)}, bf16[2,8,128,1024]{3,2,1,0:T(8,128)(2,1)}) async-done(((bf16[3,8,32,1024]{3,2,1,0:T(8,128)(2,1)}, bf16[2,8,128,1024]{3,2,1,0:T(8,128)(2,1)}), (bf16[3,8,32,1024]{3,2,1,0:T(8,128)(2,1)}, bf16[2,8,128,1024]{3,2,1,0:T(8,128)(2,1)})) %all-reduce.5.cloned.1.call-update) | async-done | bytes 5767184
  233.1 1.6 constant_dynamic-slice_fusion
  234.7 19.7 %all-gather = bf16[12,1,32,1024]{3,2,1,0:T(8,128)(2,1)S(1)} all-gather(bf16[3,1,32,1024]{3,2,1,0:T(8,128)(2,1)S(1)} %constant_dynamic-slice_fusion), channel_id=2, replica_groups=mesh['dp'=8,'mp'=4] {'mp'}, dimensions={0}, use_global_device_ids=true | all-gather | bytes 983040 | tf_op jit(solution)/shard_map/all_gather | solution.py:18
  254.4 0.2 convert_multiply_fusion
  254.6 0.0 copy-start.1
  254.6 0.2 copy.42
  254.8 0.0 copy-start
  254.8 1.0 copy-done.1
  255.8 2.8 bitcast_add_fusion.1
  258.6 0.0 copy-done
  258.6 1.4 bitcast_add_fusion
  260.1 0.0 all-to-all-done
  260.1 0.7 copy.47
  260.8 19.6 %all-gather.3.cloned.1.call-done = bf16[3072,1024]{1,0:T(8,128)(2,1)} async-done(((bf16[384,1024]{1,0:T(8,128)(2,1)}), bf16[3072,1024]{1,0:T(8,128)(2,1)}) %all-gather.3.cloned.1.call-update) | async-done | bytes 6291472 | tf_op jit(solution)/shard_map/all_gather | solution.py:77
  280.5 4.7 %fusion.5 = bf16[3,1024,256]{1,2,0:T(8,128)(2,1)S(1)} fusion(bf16[3,1024,256]{2,1,0:T(8,128)(2,1)S(1)} %bitcast.74, bf16[3,1024,1024]{2,1,0:T(8,128)(2,1)} %bitcast.75), kind=kOutput, calls=%fused_computation.15 | convolution fusion | flops 1611399168 | bytes 9437184 | tf_op jit(solution)/shard_map/kbc,kcf->kbf/dot_general | solution.py:78
  285.2 1.6 copy.49
  (4 shorter events, 0.0 us)
Async XLA Ops:
  7.2 106.9 %reduce-scatter.8.cloned.1.call-start = ((), (), s32[]{:S(2)}) async-start(), calls=%async_computation.2 | async-start | bytes 14155776 | tf_op jit(solution)/shard_map/reduce_scatter | solution.py:64
  18.9 214.2 %all-reduce.5.cloned.1.call-start = ((), (), s32[]{:S(2)}) async-start(), calls=%async_computation.4 | async-start | bytes 11534336
  19.0 3.2 %copy-start.2 = (s32[5,8]{1,0:T(8,128)S(1)}, s32[5,8]{1,0:T(8,128)}, u32[]{:S(2)}) copy-start(s32[5,8]{1,0:T(8,128)} %param.13) | copy-start | bytes 484
  48.2 232.3 %all-gather.3.cloned.1.call-start = ((), (), s32[]{:S(2)}) async-start(), calls=%async_computation.3 | async-start | bytes 7077888 | tf_op jit(solution)/shard_map/all_gather | solution.py:77
  120.1 3.7 %copy-start.3 = (u32[32]{0:T(128)S(1)}, u32[32]{0:T(128)}, u32[]{:S(2)}) copy-start(u32[32]{0:T(128)} %constant.77) | copy-start | bytes 388
  120.1 140.0 %all-to-all-start = ((bf16[384,8,256]{0,2,1:T(8,128)(2,1)}), bf16[384,8,256]{0,2,1:T(8,128)(2,1)S(1)}, u32[]{:S(2)}, u32[]{:S(2)}) async-start(bf16[384,8,256]{0,2,1:T(8,128)(2,1)} %bitcast.15), calls=%async_computation.1 | async-start | bytes 3145728 | tf_op jit(solution)/shard_map/all_to_all | solution.py:76
  254.6 1.2 copy-start.1
  254.8 3.9 %copy-start = (f32[1,3,128,1024]{3,2,1,0:T(8,128)S(1)}, f32[1,3,128,1024]{3,2,1,0:T(8,128)}, u32[]{:S(2)}) copy-start(f32[1,3,128,1024]{3,2,1,0:T(8,128)} %param.9) | copy-start | bytes 4718596
Sparse Core Ops, SparseCore 0:
  19.0 94.9 reduce-scatter.7
  118.0 114.9 all-reduce.4
  235.0 45.4 all-gather.2
